TPU v7x, 256 devices: a whole 4x4x8 slice. The times are simulated.
256 devices in a mesh: bx: 16 (over x, y), by: 16 (over z, core).
Axes of the slice: x: 4, y: 4, z: 8, core: 2. Of those that a mesh axis runs over, the one named last changes fastest.
Arguments:
- forcing: float32 [2432, 4096], P('by', 'bx'), may hold values from -20 to 20
- guess: float32 [2432, 4096], P('by', 'bx'), may hold values from -3 to 3
- shift: float32 [2432, 4096], P('by', 'bx'), may hold values from 0.05 to 2
- ocean_mask: int32 [2432, 4096], P('by', 'bx'), may hold values 0 or 1
Outputs:
- solution_field: float32 [2432, 4096], P('by', 'bx')
- residual: float32 [2432, 4096], P('by', 'bx')
- residual_norm: float32 [], replicated
All inputs are finite; a program needn't handle non-finite values. No bound on the sum of `ocean_mask` on one device may be relied on, other than what follows from the above.
Results may differ from a plain program's by a relative error of at most 0.00002.
Values sent between devices are 32-bit elements; how exact they have to be, the bound alone decides.
A program may use at most 64 MiB of HBM per device.

v0:
```python
import jax
import jax.numpy as jnp
from jax import lax
from jax.sharding import PartitionSpec as P

ITERS = 4
LOW_BOUND = 0.05
HIGH_BOUND = 14.5


def padded_2(block, sides, width):
    for axis, dim in sides:
        count = lax.axis_size(axis)
        forward = [(i, i + 1) for i in range(count - 1)]
        forward.append((count - 1, 0))
        backward = [(target, source) for source, target in forward]
        low = lax.ppermute(
            lax.slice_in_dim(block, block.shape[dim] - width, None, axis=dim), axis, forward
        )
        high = lax.ppermute(lax.slice_in_dim(block, 0, width, axis=dim), axis, backward)
        block = jnp.concatenate([low, block, high], axis=dim)
    return block


def sent_to_all(x, axis):
    copies = jnp.broadcast_to(x, (lax.axis_size(axis), *x.shape))
    return lax.all_to_all(copies, axis, split_axis=0, concat_axis=0, tiled=True)


def laid_out(tiles, dim):
    tiles = jnp.moveaxis(tiles, 0, dim)
    dims = tiles.shape
    return tiles.reshape(*dims[:dim], dims[dim] * dims[dim + 1], *dims[dim + 2 :])


def gather_directly(x, axis, dim):
    tiles = sent_to_all(x, axis)
    return laid_out(tiles, dim)


def gather_turned(arrays, axis, dims):
    turned = [jnp.moveaxis(a, dim, 0) for a, dim in zip(arrays, dims)]
    both = jnp.concatenate([t.reshape(len(t), -1) for t in turned], axis=1)
    filled, at, outs = (lax.all_gather(both, axis, axis=0, tiled=True), 0, [])
    for t, dim in zip(turned, dims):
        piece = filled[:, at : at + t[0].size].reshape(-1, *t.shape[1:])
        outs.append(jnp.moveaxis(piece, 0, dim))
        at += t[0].size
    return tuple(outs)


def stencil_padded(padded, shift, mask_f):
    center = padded[1:-1, 1:-1]
    sides = padded[2:, 1:-1] + padded[:-2, 1:-1] + padded[1:-1, 2:] + padded[1:-1, :-2]
    corners = padded[2:, 2:] + padded[2:, :-2] + padded[:-2, 2:] + padded[:-2, :-2]
    return mask_f * ((6.0 + shift) * center - sides - 0.5 * corners)


def crop_cycle(values, cycle):
    return values[cycle : values.shape[0] - cycle, cycle : values.shape[1] - cycle]


def local_stencil(values, shift_full, mask_full):
    cycle = (shift_full.shape[0] - values.shape[0]) // 2 + 1
    return stencil_padded(values, crop_cycle(shift_full, cycle), crop_cycle(mask_full, cycle))


def deep_inputs(forcing, guess, shift, mask_f):
    rows, cols = forcing.shape
    depth = ITERS + 1
    stacked = jnp.stack([forcing, guess, shift, mask_f])
    padded = padded_2(stacked, (("bx", 2), ("by", 1)), depth)
    top_rows = stacked[:, rows - depth :, :]
    whole_top = gather_directly(top_rows, "bx", 2)
    flipped = whole_top[:, ::-1, ::-1]
    extended = jnp.concatenate([flipped[:, :, -depth:], flipped, flipped[:, :, :depth]], axis=2)
    ghost = lax.dynamic_slice_in_dim(extended, lax.axis_index("bx") * cols, cols + 2 * depth, 2)
    row_index = lax.axis_index("by")
    upper_rows = jnp.where(row_index == lax.axis_size("by") - 1, ghost, padded[:, rows + depth :])
    lower_rows = jnp.where(row_index == 0, jnp.zeros_like(ghost), padded[:, :depth])
    return jnp.concatenate([lower_rows, padded[:, depth : rows + depth], upper_rows], axis=1)


def pair_add(first, second):
    total = first[0] + second[0]
    backed = total - first[0]
    error = first[0] - (total - backed) + (second[0] - backed)
    error = error + first[1] + second[1]
    upper = total + error
    lower = error - (upper - total)
    return (upper, lower)


def tree_total(uppers, lowers):
    while uppers.shape[0] > 1:
        if uppers.shape[0] % 2 == 1:
            uppers = jnp.concatenate([uppers, jnp.zeros((1,), uppers.dtype)])
            lowers = jnp.concatenate([lowers, jnp.zeros((1,), lowers.dtype)])
        uppers, lowers = pair_add((uppers[0::2], lowers[0::2]), (uppers[1::2], lowers[1::2]))
    return (uppers[0], lowers[0])


def per_device(forcing, guess, shift, ocean_mask):
    mask_f = ocean_mask.astype(jnp.float32)
    theta = (HIGH_BOUND + LOW_BOUND) / 2.0
    delta = (HIGH_BOUND - LOW_BOUND) / 2.0
    sigma = theta / delta
    rho = 1.0 / sigma
    full = deep_inputs(forcing, guess, shift, mask_f)
    forcing_full = full[0]
    guess_full = full[1]
    shift_full = full[2]
    mask_full = full[3]
    iterate = mask_full * guess_full
    resid = crop_cycle(mask_full * forcing_full, 1) - local_stencil(iterate, shift_full, mask_full)
    direction = resid / theta
    iterate = crop_cycle(iterate, 1)
    for sweep in range(ITERS):
        iterate = iterate + direction
        image = local_stencil(direction, shift_full, mask_full)
        resid = crop_cycle(resid, 1) - image
        rho_next = 1.0 / (2.0 * sigma - rho)
        direction = rho_next * rho * crop_cycle(direction, 1) + 2.0 * rho_next / delta * resid
        rho = rho_next
        iterate = crop_cycle(iterate, 1)
    row_sums = jnp.sum(resid * resid, axis=1)
    upper, lower = tree_total(row_sums, jnp.zeros_like(row_sums))
    all_upper, all_lower = gather_turned((upper[None], lower[None]), ("bx", "by"), (0, 0))
    upper, lower = tree_total(all_upper, all_lower)
    grid_cells = resid.shape[0] * lax.axis_size("by") * resid.shape[1] * lax.axis_size("bx")
    norm_value = jnp.sqrt((upper + lower) / grid_cells)
    return (iterate, resid, norm_value)


def solution(mesh):
    in_specs = (P("by", "bx"), P("by", "bx"), P("by", "bx"), P("by", "bx"))
    out_specs = (P("by", "bx"), P("by", "bx"), P())
    return jax.shard_map(
        per_device, mesh=mesh, in_specs=in_specs, out_specs=out_specs, check_vma=False
    )
```

profile of v0, /device:TPU:1, one launch (start us, length us, event | category | flops | bytes accessed | tf_op | source)
XLA Modules:
  0.0 117.5 jit_solution(8575989142189107592)
XLA Ops:
  0.6 1.1 stack.15
  1.8 0.8 copy-done.1
  2.7 0.8 copy-done.2
  3.7 0.6 pad_maximum_fusion.1
  4.3 0.2 fusion.39
  4.5 2.2 %collective-permute-start = (f32[4,152,5]{2,0,1:T(4,128)S(1)}, f32[4,152,5]{2,0,1:T(4,128)S(1)}, u32[]{:S(2)}, u32[]{:S(2)}) collective-permute-start(f32[4,152,5]{2,0,1:T(4,128)S(1)} %get-tuple-element.75), channel_id=1, source_target_pairs={{0,16},{16,32},{32,48},{48,64},{64,80},{80,96},{96,112},{112,128},... | collective-permute-start | bytes 36488 | tf_op jit(solution)/shard_map/ppermute | solution.py:17
  6.7 3.7 %collective-permute-start.1 = (f32[4,152,5]{2,0,1:T(4,128)S(1)}, f32[4,152,5]{2,0,1:T(4,128)S(1)}, u32[]{:S(2)}, u32[]{:S(2)}) collective-permute-start(f32[4,152,5]{2,0,1:T(4,128)S(1)} %get-tuple-element.76), channel_id=1, source_target_pairs={{16,0},{32,16},{48,32},{64,48},{80,64},{96,80},{112,96},{128,112},... | collective-permute-start | bytes 36488 | tf_op jit(solution)/shard_map/ppermute | solution.py:20
  10.4 0.8 broadcast_in_dim.7
  11.2 3.5 %all-to-all-start = ((f32[16,4,5,256]{3,1,2,0:T(4,128)}), f32[16,4,5,256]{3,1,2,0:T(4,128)S(1)}, u32[]{:S(2)}, u32[]{:S(2)}) async-start(f32[16,4,5,256]{3,1,2,0:T(4,128)} %broadcast_in_dim.7), calls=%async_computation | async-start | bytes 655360 | tf_op jit(solution)/shard_map/all_to_all | solution.py:27
  14.8 0.8 collective-permute-done
  15.5 0.2 pad_maximum_fusion.7
  15.8 6.2 %collective-permute-start.2 = (f32[4,5,266]{2,0,1:T(4,128)S(1)}, f32[4,5,266]{2,0,1:T(4,128)S(1)}, u32[]{:S(2)}, u32[]{:S(2)}) collective-permute-start(f32[4,5,266]{2,0,1:T(4,128)S(1)} %get-tuple-element.69), channel_id=1, source_target_pairs={{0,1},{1,2},{2,3},{3,4},{4,5},{5,6},{6,7},{7,8},{8,9},{9,10},{10,1... | collective-permute-start | bytes 63848 | tf_op jit(solution)/shard_map/ppermute | solution.py:17
  22.0 1.0 collective-permute-done.2
  23.1 3.1 %rev.3 = f32[4,5,4096]{2,0,1:T(4,128)S(1)} reverse(f32[4,5,4096]{2,0,1:T(4,128)S(1)} %bitcast.28), dimensions={1,2} | reverse | bytes 655360 | tf_op jit(solution)/shard_map/rev | solution.py:75
  26.3 0.4 concatenate.31
  26.9 2.3 %pad_maximum_fusion = f32[4,162,266]{2,0,1:T(4,128)S(1)} fusion(f32[4,5,266]{2,0,1:T(4,128)S(1)} %dynamic-slice_select_fusion, f32[4,152,5]{2,0,1:T(4,128)S(1)} %collective-permute-done.1, f32[1,152,256]{2,0,1:T(1,128)S(1)} %stack.18, f32[1,152,256]{2,0,1:T(1,128)S(1)} %stack.17, f32[1,152,256]{2,0,1:T(1,128)S(1)} %stack.16, f32[1,152,256]{2,0,1:T(1,128)S(1)} %stack.15, ...), kind=kLoop, calls=%fused_computation | loop fusion | flops 1206576 | bytes 1378944 | tf_op jit(solution)/shard_map/concatenate | solution.py:81
  29.2 0.7 fusion.38
  30.2 0.7 broadcast_multiply_fusion
  31.0 0.6 multiply_add_fusion.2
  31.8 0.6 multiply_add_fusion.1
  32.4 0.6 multiply_add_fusion
  33.1 1.4 %multiply_reduce_fusion = (f32[152]{0:T(256)S(1)}, f32[152,256]{1,0:T(8,128)}, f32[152,256]{1,0:T(8,128)}) fusion(f32[154,258]{1,0:T(8,128)S(1)} %get-tuple-element.61, f32[162,266]{1,0:T(8,128)S(1)} %bitcast.26, f32[162,266]{1,0:T(8,128)S(1)} %get-tuple-element.90, f32[154,258]{1,0:T(8,128)S(1)} %get-tuple-element.62, f32[154,258]{1,0:T(8,128)S(1)} %get-tuple-element.80, ...), kind=kLoop, calls=%fused_computation.80 | loop fusion | flops 739176 | bytes 2802272 | tf_op jit(solution)/shard_map/reduce_sum | solution.py:126
  38.0 0.6 fusion.44
  41.0 0.6 fusion.43
  43.5 63.3 %all-gather = f32[256,1,2]{2,1,0:T(1,128)S(1)} all-gather(f32[1,1,2]{2,1,0:T(1,128)S(1)} %maximum_bitcast_fusion), channel_id=1, replica_groups=mesh['bx'=16,'by'=16] {'bx','by'}, dimensions={0}, use_global_device_ids=true | all-gather | bytes 2056 | tf_op jit(solution)/shard_map/all_gather | solution.py:44
  106.8 0.2 slice_reduce_fusion
  107.1 0.2 slice.547
  107.3 0.2 slice.546
  107.5 0.2 slice.544
  107.7 0.2 slice.543
  110.9 0.6 fusion.42
  113.9 0.6 fusion.41
  (110 shorter events, 7.6 us)
Async XLA Ops:
  0.6 1.1 copy-start
  1.7 0.9 copy-start.1
  2.6 0.9 copy-start.2
  4.5 11.0 %collective-permute-start = (f32[4,152,5]{2,0,1:T(4,128)S(1)}, f32[4,152,5]{2,0,1:T(4,128)S(1)}, u32[]{:S(2)}, u32[]{:S(2)}) collective-permute-start(f32[4,152,5]{2,0,1:T(4,128)S(1)} %get-tuple-element.75), channel_id=1, source_target_pairs={{0,16},{16,32},{32,48},{48,64},{64,80},{80,96},{96,112},{112,128},... | collective-permute-start | bytes 36488 | tf_op jit(solution)/shard_map/ppermute | solution.py:17
  6.7 8.9 %collective-permute-start.1 = (f32[4,152,5]{2,0,1:T(4,128)S(1)}, f32[4,152,5]{2,0,1:T(4,128)S(1)}, u32[]{:S(2)}, u32[]{:S(2)}) collective-permute-start(f32[4,152,5]{2,0,1:T(4,128)S(1)} %get-tuple-element.76), channel_id=1, source_target_pairs={{16,0},{32,16},{48,32},{64,48},{80,64},{96,80},{112,96},{128,112},... | collective-permute-start | bytes 36488 | tf_op jit(solution)/shard_map/ppermute | solution.py:20
  11.2 11.7 %all-to-all-start = ((f32[16,4,5,256]{3,1,2,0:T(4,128)}), f32[16,4,5,256]{3,1,2,0:T(4,128)S(1)}, u32[]{:S(2)}, u32[]{:S(2)}) async-start(f32[16,4,5,256]{3,1,2,0:T(4,128)} %broadcast_in_dim.7), calls=%async_computation | async-start | bytes 655360 | tf_op jit(solution)/shard_map/all_to_all | solution.py:27
  15.8 7.2 %collective-permute-start.2 = (f32[4,5,266]{2,0,1:T(4,128)S(1)}, f32[4,5,266]{2,0,1:T(4,128)S(1)}, u32[]{:S(2)}, u32[]{:S(2)}) collective-permute-start(f32[4,5,266]{2,0,1:T(4,128)S(1)} %get-tuple-element.69), channel_id=1, source_target_pairs={{0,1},{1,2},{2,3},{3,4},{4,5},{5,6},{6,7},{7,8},{8,9},{9,10},{10,1... | collective-permute-start | bytes 63848 | tf_op jit(solution)/shard_map/ppermute | solution.py:17
  22.0 4.8 %collective-permute-start.3 = (f32[4,5,266]{2,0,1:T(4,128)S(1)}, f32[4,5,266]{2,0,1:T(4,128)S(1)}, u32[]{:S(2)}, u32[]{:S(2)}) collective-permute-start(f32[4,5,266]{2,0,1:T(4,128)S(1)} %get-tuple-element.70), channel_id=1, source_target_pairs={{1,0},{2,1},{3,2},{4,3},{5,4},{6,5},{7,6},{8,7},{9,8},{10,9},{11,1... | collective-permute-start | bytes 63848 | tf_op jit(solution)/shard_map/ppermute | solution.py:20
where the time goes:
time: 118 us
  blocking collectives  63.3 us (54%)
  local copies, waits for them, and re-layouts  17.9 us (15%)
  starting transfers between devices  15.7 us (13%)
  between operations  10.8 us (9%)
  other arithmetic  8.12 us (7%)
  waiting for transfers between devices  1.77 us (2%)
    all_gather x1, blocking collectives, gather_turned(): filled, at, outs = (lax.all_gather(both, axis, axis=0, tiled=True), 0, [])  63.3 us
    ppermute x2, starting transfers between devices, padded_2(): lax.ppermute(lax.slice_in_dim(block, block.shape[dim] - width, None, axis...  8.39 us
    ppermute x2, starting transfers between devices, padded_2(): lax.ppermute(lax.slice_in_dim(block, 0, width, axis=dim), axis, backward)  3.73 us
    all_to_all x1, starting transfers between devices, sent_to_all(): return lax.all_to_all(copies, axis, split_axis=0, concat_axis=0, tiled=True)  3.54 us
    rev x1, local copies, waits for them, and re-layouts, deep_inputs(): flipped = whole_top[:, ::-1, ::-1]  3.06 us
    slice x16, local copies, waits for them, and re-layouts, tree_total(): uppers[1::2]  2.87 us
    slice x15, local copies, waits for them, and re-layouts, tree_total(): lowers[1::2]  2.7 us
  transfers between devices with their start and end apart: 5, of which 2 were waited for; matrix products, arithmetic and copies ran while one was open for 4% of the time, Pallas kernels for 0%

commit v1 on v0

--- a/solution.py
+++ b/solution.py
@@ -41,7 +41,13 @@
 def gather_turned(arrays, axis, dims):
     turned = [jnp.moveaxis(a, dim, 0) for a, dim in zip(arrays, dims)]
     both = jnp.concatenate([t.reshape(len(t), -1) for t in turned], axis=1)
-    filled, at, outs = (lax.all_gather(both, axis, axis=0, tiled=True), 0, [])
+    filled, at, outs = (
+        jnp.concatenate(
+            lax.all_to_all(jnp.stack([both] * lax.axis_size(axis)), axis, 0, 0), axis=0
+        ),
+        0,
+        [],
+    )
     for t, dim in zip(turned, dims):
         piece = filled[:, at : at + t[0].size].reshape(-1, *t.shape[1:])
         outs.append(jnp.moveaxis(piece, 0, dim))

time: 118 us -> 84.7 us (0.72)
  blocking collectives: 63.3 us -> 30 us
    all_gather x1 -> x0, blocking collectives: 63.3 us -> none  [gather_turned(): filled, at, outs = (lax.all_gather(both, axis, axis=0, tiled=True), 0, [])]
    all_to_all x0 -> x1, blocking collectives: none -> 30 us  [gather_turned(): lax.all_to_all(jnp.stack([both] * lax.axis_size(axis)), axis, 0, 0)]
  transfers between devices with their start and end apart: 5 -> 5, of which waited for: 2 -> 2; matrix products, arithmetic and copies ran while one was open for 4% -> 6% of each run, Pallas kernels for 0% -> 0%
where the time goes in v1:
time: 84.7 us; the launch traced here: 84.3 us
  blocking collectives  30 us (35%)
  local copies, waits for them, and re-layouts  18 us (21%)
  starting transfers between devices  15.7 us (19%)
  between operations  10.8 us (13%)
  other arithmetic  8.12 us (10%)
  waiting for transfers between devices  1.77 us (2%)
    all_to_all x1, blocking collectives, gather_turned(): lax.all_to_all(jnp.stack([both] * lax.axis_size(axis)), axis, 0, 0)  30 us
    ppermute x2, starting transfers between devices, padded_2(): lax.ppermute(lax.slice_in_dim(block, block.shape[dim] - width, None, axis...  8.39 us
    ppermute x2, starting transfers between devices, padded_2(): lax.ppermute(lax.slice_in_dim(block, 0, width, axis=dim), axis, backward)  3.73 us
    all_to_all x1, starting transfers between devices, sent_to_all(): return lax.all_to_all(copies, axis, split_axis=0, concat_axis=0, tiled=True)  3.54 us
    rev x1, local copies, waits for them, and re-layouts, deep_inputs(): flipped = whole_top[:, ::-1, ::-1]  3.06 us
    slice x16, local copies, waits for them, and re-layouts, tree_total(): uppers[1::2]  2.87 us
    slice x15, local copies, waits for them, and re-layouts, tree_total(): lowers[1::2]  2.7 us
    concatenate x1, other arithmetic, deep_inputs(): jnp.concatenate([lower_rows, padded[:, depth:rows + depth], upper_rows],...  2.33 us
  transfers between devices with their start and end apart: 5, of which 2 were waited for; matrix products, arithmetic and copies ran while one was open for 6% of the time, Pallas kernels for 0%

profile of v1, /device:TPU:1, one launch (start us, length us, event | category | flops | bytes accessed | tf_op | source)
XLA Modules:
  0.0 84.3 jit_solution(11696094138121313663)
XLA Ops:
  0.6 1.1 %stack.12 = f32[1,152,256]{2,0,1:T(1,128)S(1)} reshape(f32[152,256]{1,0:T(8,128)} %param.4) | data formatting | bytes 311296 | tf_op jit(solution)/shard_map/stack | solution.py:77
  1.8 0.8 copy-done.1
  2.7 0.8 copy-done.2
  3.7 0.6 pad_maximum_fusion.1
  4.3 0.2 fusion.39
  4.5 2.2 %collective-permute-start = (f32[4,152,5]{2,0,1:T(4,128)S(1)}, f32[4,152,5]{2,0,1:T(4,128)S(1)}, u32[]{:S(2)}, u32[]{:S(2)}) collective-permute-start(f32[4,152,5]{2,0,1:T(4,128)S(1)} %get-tuple-element.75), channel_id=1, source_target_pairs={{0,16},{16,32},{32,48},{48,64},{64,80},{80,96},{96,112},{112,128},... | collective-permute-start | bytes 36488 | tf_op jit(solution)/shard_map/ppermute | solution.py:17
  6.7 3.7 %collective-permute-start.1 = (f32[4,152,5]{2,0,1:T(4,128)S(1)}, f32[4,152,5]{2,0,1:T(4,128)S(1)}, u32[]{:S(2)}, u32[]{:S(2)}) collective-permute-start(f32[4,152,5]{2,0,1:T(4,128)S(1)} %get-tuple-element.76), channel_id=1, source_target_pairs={{16,0},{32,16},{48,32},{64,48},{80,64},{96,80},{112,96},{128,112},... | collective-permute-start | bytes 36488 | tf_op jit(solution)/shard_map/ppermute | solution.py:20
  10.4 0.8 broadcast_in_dim.7
  11.2 3.5 %all-to-all-start = ((f32[16,4,5,256]{3,1,2,0:T(4,128)}), f32[16,4,5,256]{3,1,2,0:T(4,128)S(1)}, u32[]{:S(2)}, u32[]{:S(2)}) async-start(f32[16,4,5,256]{3,1,2,0:T(4,128)} %broadcast_in_dim.7), calls=%async_computation | async-start | bytes 655360 | tf_op jit(solution)/shard_map/all_to_all | solution.py:27
  14.8 0.8 collective-permute-done
  15.5 0.2 pad_maximum_fusion.7
  15.8 6.2 %collective-permute-start.2 = (f32[4,5,266]{2,0,1:T(4,128)S(1)}, f32[4,5,266]{2,0,1:T(4,128)S(1)}, u32[]{:S(2)}, u32[]{:S(2)}) collective-permute-start(f32[4,5,266]{2,0,1:T(4,128)S(1)} %get-tuple-element.69), channel_id=1, source_target_pairs={{0,1},{1,2},{2,3},{3,4},{4,5},{5,6},{6,7},{7,8},{8,9},{9,10},{10,1... | collective-permute-start | bytes 63848 | tf_op jit(solution)/shard_map/ppermute | solution.py:17
  22.0 1.0 %collective-permute-done.2 = f32[4,5,266]{2,0,1:T(4,128)S(1)} collective-permute-done((f32[4,5,266]{2,0,1:T(4,128)S(1)}, f32[4,5,266]{2,0,1:T(4,128)S(1)}, u32[]{:S(2)}, u32[]{:S(2)}) %collective-permute-start.2) | collective-permute-done | bytes 21312 | tf_op jit(solution)/shard_map/ppermute | solution.py:17
  23.1 3.1 %rev.3 = f32[4,5,4096]{2,0,1:T(4,128)S(1)} reverse(f32[4,5,4096]{2,0,1:T(4,128)S(1)} %bitcast.28), dimensions={1,2} | reverse | bytes 655360 | tf_op jit(solution)/shard_map/rev | solution.py:81
  26.3 0.4 concatenate.33
  26.9 2.3 %pad_maximum_fusion = f32[4,162,266]{2,0,1:T(4,128)S(1)} fusion(f32[4,5,266]{2,0,1:T(4,128)S(1)} %dynamic-slice_select_fusion, f32[4,152,5]{2,0,1:T(4,128)S(1)} %collective-permute-done.1, f32[1,152,256]{2,0,1:T(1,128)S(1)} %stack.15, f32[1,152,256]{2,0,1:T(1,128)S(1)} %stack.14, f32[1,152,256]{2,0,1:T(1,128)S(1)} %stack.13, f32[1,152,256]{2,0,1:T(1,128)S(1)} %stack.12, ...), kind=kLoop, calls=%fused_computation | loop fusion | flops 1206576 | bytes 1378944 | tf_op jit(solution)/shard_map/concatenate | solution.py:87
  29.2 0.7 fusion.38
  30.2 0.7 broadcast_multiply_fusion
  31.0 0.6 multiply_add_fusion.2
  31.8 0.6 multiply_add_fusion.1
  32.4 0.6 multiply_add_fusion
  33.1 1.4 %multiply_reduce_fusion = (f32[152]{0:T(256)S(1)}, f32[152,256]{1,0:T(8,128)}, f32[152,256]{1,0:T(8,128)}) fusion(f32[154,258]{1,0:T(8,128)S(1)} %get-tuple-element.61, f32[162,266]{1,0:T(8,128)S(1)} %bitcast.26, f32[162,266]{1,0:T(8,128)S(1)} %get-tuple-element.90, f32[154,258]{1,0:T(8,128)S(1)} %get-tuple-element.62, f32[154,258]{1,0:T(8,128)S(1)} %get-tuple-element.80, ...), kind=kLoop, calls=%fused_computation.80 | loop fusion | flops 739176 | bytes 2802272 | tf_op jit(solution)/shard_map/reduce_sum | solution.py:132
  38.0 0.6 fusion.44
  41.0 0.6 fusion.43
  43.6 30.0 %all_to_all.10 = f32[256,1,2]{2,1,0:T(1,128)S(1)} all-to-all(f32[256,1,2]{2,1,0:T(1,128)S(1)} %stack.17), channel_id=1, replica_groups=mesh['bx'=16,'by'=16] {'bx','by'}, dimensions={0} | all-to-all | bytes 4096 | tf_op jit(solution)/shard_map/all_to_all | solution.py:46
  73.6 0.2 slice_reduce_fusion
  73.9 0.2 slice.547
  74.1 0.2 slice.546
  74.3 0.2 slice.544
  74.5 0.2 slice.543
  77.7 0.6 fusion.42
  80.7 0.6 fusion.41
  (111 shorter events, 7.7 us)
Async XLA Ops:
  0.6 1.1 %copy-start = (f32[152,256]{1,0:T(8,128)S(1)}, f32[152,256]{1,0:T(8,128)}, u32[]{:S(2)}) copy-start(f32[152,256]{1,0:T(8,128)} %param.5) | copy-start | bytes 466948
  1.7 0.9 %copy-start.1 = (f32[152,256]{1,0:T(8,128)S(1)}, f32[152,256]{1,0:T(8,128)}, u32[]{:S(2)}) copy-start(f32[152,256]{1,0:T(8,128)} %param.6) | copy-start | bytes 466948
  2.6 0.9 %copy-start.2 = (s32[152,256]{1,0:T(8,128)S(1)}, s32[152,256]{1,0:T(8,128)}, u32[]{:S(2)}) copy-start(s32[152,256]{1,0:T(8,128)} %param.7) | copy-start | bytes 466948
  4.5 11.0 %collective-permute-start = (f32[4,152,5]{2,0,1:T(4,128)S(1)}, f32[4,152,5]{2,0,1:T(4,128)S(1)}, u32[]{:S(2)}, u32[]{:S(2)}) collective-permute-start(f32[4,152,5]{2,0,1:T(4,128)S(1)} %get-tuple-element.75), channel_id=1, source_target_pairs={{0,16},{16,32},{32,48},{48,64},{64,80},{80,96},{96,112},{112,128},... | collective-permute-start | bytes 36488 | tf_op jit(solution)/shard_map/ppermute | solution.py:17
  6.7 8.9 %collective-permute-start.1 = (f32[4,152,5]{2,0,1:T(4,128)S(1)}, f32[4,152,5]{2,0,1:T(4,128)S(1)}, u32[]{:S(2)}, u32[]{:S(2)}) collective-permute-start(f32[4,152,5]{2,0,1:T(4,128)S(1)} %get-tuple-element.76), channel_id=1, source_target_pairs={{16,0},{32,16},{48,32},{64,48},{80,64},{96,80},{112,96},{128,112},... | collective-permute-start | bytes 36488 | tf_op jit(solution)/shard_map/ppermute | solution.py:20
  11.2 11.7 %all-to-all-start = ((f32[16,4,5,256]{3,1,2,0:T(4,128)}), f32[16,4,5,256]{3,1,2,0:T(4,128)S(1)}, u32[]{:S(2)}, u32[]{:S(2)}) async-start(f32[16,4,5,256]{3,1,2,0:T(4,128)} %broadcast_in_dim.7), calls=%async_computation | async-start | bytes 655360 | tf_op jit(solution)/shard_map/all_to_all | solution.py:27
  15.8 7.2 %collective-permute-start.2 = (f32[4,5,266]{2,0,1:T(4,128)S(1)}, f32[4,5,266]{2,0,1:T(4,128)S(1)}, u32[]{:S(2)}, u32[]{:S(2)}) collective-permute-start(f32[4,5,266]{2,0,1:T(4,128)S(1)} %get-tuple-element.69), channel_id=1, source_target_pairs={{0,1},{1,2},{2,3},{3,4},{4,5},{5,6},{6,7},{7,8},{8,9},{9,10},{10,1... | collective-permute-start | bytes 63848 | tf_op jit(solution)/shard_map/ppermute | solution.py:17
  22.0 4.8 %collective-permute-start.3 = (f32[4,5,266]{2,0,1:T(4,128)S(1)}, f32[4,5,266]{2,0,1:T(4,128)S(1)}, u32[]{:S(2)}, u32[]{:S(2)}) collective-permute-start(f32[4,5,266]{2,0,1:T(4,128)S(1)} %get-tuple-element.70), channel_id=1, source_target_pairs={{1,0},{2,1},{3,2},{4,3},{5,4},{6,5},{7,6},{8,7},{9,8},{10,9},{11,1... | collective-permute-start | bytes 63848 | tf_op jit(solution)/shard_map/ppermute | solution.py:20
